TPU v7x, 32 devices: a whole 2x2x4 slice. The times are simulated.
32 devices in a mesh: dp: 2 (over x), pp: 4 (over z), ep: 4 (over y, core).
Axes of the slice: x: 2, y: 2, z: 4, core: 2. Of those that a mesh axis runs over, the one named last changes fastest.
Arguments:
- hidden_in: bfloat16 [24, 128, 1024], P(None, ('dp', 'ep')), parts along dimension 1
- seq_pos: int32 [24, 128], P(None, ('dp', 'ep')), parts along dimension 1
- k_cache: bfloat16 [4, 24, 128, 16, 8, 64], P('pp', None, ('dp', 'ep')), parts along dimension 2
- v_cache: bfloat16 [4, 24, 128, 16, 8, 64], P('pp', None, ('dp', 'ep')), parts along dimension 2
- expert_ids: int32 [4, 24, 128, 8], P('pp', None, ('dp', 'ep')), parts along dimension 2
- w_query: bfloat16 [4, 1024, 1024], P('pp')
- w_key: bfloat16 [4, 1024, 512], P('pp')
- w_value: bfloat16 [4, 1024, 512], P('pp')
- w_out: bfloat16 [4, 1024, 1024], P('pp')
- attn_gain: bfloat16 [4, 1024], P('pp')
- mlp_gain: bfloat16 [4, 1024], P('pp')
- w_router: bfloat16 [4, 1024, 32], P('pp')
- w_gate: bfloat16 [4, 32, 1024, 512], P('pp', 'ep')
- w_up: bfloat16 [4, 32, 1024, 512], P('pp', 'ep')
- w_down: bfloat16 [4, 32, 512, 1024], P('pp', 'ep')
- final_gain: bfloat16 [1024], replicated
Outputs:
- output 1: bfloat16 [24, 128, 1024], P(None, ('dp', 'ep')), parts along dimension 1
- output 2: bfloat16 [4, 24, 128, 8, 64], P('pp', None, ('dp', 'ep')), parts along dimension 2
- output 3: bfloat16 [4, 24, 128, 8, 64], P('pp', None, ('dp', 'ep')), parts along dimension 2
There are 2 independent parts. A program takes and returns all parts, laid end to end along the dimension named above; an argument that names none is the same for every part.
All inputs are finite; a program needn't handle non-finite values.
Results may differ from a plain program's by a relative error of at most 0.02.
Values are sent between devices in bfloat16 or wider.
A program may use at most 1 GiB of HBM per device.

v0:
```python
import jax
import jax.numpy as jnp
from jax import lax
from jax.sharding import PartitionSpec as P

THETA = 1000000.0
EPS = 1e-05


def rms_norm(in_vals, gain_vec):
    vals_f32 = in_vals.astype(jnp.float32)
    inv_rms = lax.rsqrt(jnp.mean(vals_f32 * vals_f32, axis=-1, keepdims=True) + EPS)
    return (vals_f32 * inv_rms * gain_vec.astype(jnp.float32)).astype(jnp.bfloat16)


def rotate(head_vecs, positions):
    half_dim = head_vecs.shape[-1] // 2
    inv_freq = THETA ** (-jnp.arange(half_dim, dtype=jnp.float32) / half_dim)
    angles = positions.astype(jnp.float32)[:, None, None] * inv_freq
    cos_ang = jnp.cos(angles)
    sin_ang = jnp.sin(angles)
    first_half = head_vecs[..., :half_dim].astype(jnp.float32)
    second_half = head_vecs[..., half_dim:].astype(jnp.float32)
    return jnp.concatenate([first_half * cos_ang - second_half * sin_ang, second_half * cos_ang + first_half * sin_ang], axis=-1).astype(jnp.bfloat16)


def attend(q_heads, key_new, val_new, k_rows, v_rows, positions):
    tokens, kv_heads, head_dim = key_new.shape
    ctx_len = k_rows.shape[1]
    q_groups = q_heads.reshape(tokens, kv_heads, -1, head_dim)
    score_scale = head_dim ** -0.5
    cache_scores = jnp.einsum("bkgh,btkh->bkgt", q_groups, k_rows, preferred_element_type=jnp.float32) * score_scale
    is_valid = jnp.arange(ctx_len)[None, None, None, :] < positions[:, None, None, None]
    cache_scores = jnp.where(is_valid, cache_scores, -jnp.inf)
    self_score = jnp.einsum("bkgh,bkh->bkg", q_groups, key_new, preferred_element_type=jnp.float32)[..., None] * score_scale
    top_score = jnp.maximum(jnp.max(cache_scores, axis=-1, keepdims=True), self_score)
    cache_w = jnp.exp(cache_scores - top_score)
    self_w = jnp.exp(self_score - top_score)
    weight_sum = jnp.sum(cache_w, axis=-1, keepdims=True) + self_w
    cache_w = (cache_w / weight_sum).astype(jnp.bfloat16)
    self_w = (self_w / weight_sum).astype(jnp.bfloat16)
    attn_out = jnp.einsum("bkgt,btkh->bkgh", cache_w, v_rows, preferred_element_type=jnp.float32) + self_w.astype(jnp.float32) * val_new.astype(jnp.float32)[:, :, None, :]
    return attn_out.astype(jnp.bfloat16).reshape(tokens, -1)


def attn_block(hidden, positions, k_rows, v_rows, w_q, w_k, w_v, w_o, gain_vec):
    tokens = hidden.shape[0]
    kv_heads, head_dim = k_rows.shape[2], k_rows.shape[3]
    normed = rms_norm(hidden, gain_vec)
    q_heads = jnp.dot(normed, w_q, preferred_element_type=jnp.float32).astype(jnp.bfloat16).reshape(tokens, -1, head_dim)
    key_new = jnp.dot(normed, w_k, preferred_element_type=jnp.float32).astype(jnp.bfloat16).reshape(tokens, kv_heads, head_dim)
    val_new = jnp.dot(normed, w_v, preferred_element_type=jnp.float32).astype(jnp.bfloat16).reshape(tokens, kv_heads, head_dim)
    q_heads = rotate(q_heads, positions)
    key_new = rotate(key_new, positions)
    attn_out = attend(q_heads, key_new, val_new, k_rows, v_rows, positions)
    hidden = (hidden.astype(jnp.float32) + jnp.dot(attn_out, w_o, preferred_element_type=jnp.float32)).astype(jnp.bfloat16)
    return hidden, key_new, val_new


def row_capacity(tokens, top_k, ep_size):
    return tokens // 2 * ((top_k + ep_size - 1) // ep_size) + tokens * top_k // (2 * ep_size)


def expert_rows(in_rows, labels, gate_col, w_g, w_u, w_d):
    local_count = w_g.shape[0]
    sort_order = jnp.argsort(labels, stable=True)
    group_sizes = jnp.sum(labels[:, None] == jnp.arange(local_count)[None, :], axis=0).astype(jnp.int32)
    sorted_rows = in_rows[sort_order]
    gate_h = lax.ragged_dot(sorted_rows, w_g, group_sizes, preferred_element_type=jnp.float32)
    up_h = lax.ragged_dot(sorted_rows, w_u, group_sizes, preferred_element_type=jnp.float32)
    act_rows = (jax.nn.silu(gate_h) * up_h).astype(jnp.bfloat16)
    down_h = lax.ragged_dot(act_rows, w_d, group_sizes, preferred_element_type=jnp.float32)
    in_group = (labels < local_count)[sort_order]
    weighted = jnp.where(in_group[:, None], gate_col[sort_order][:, None] * down_h, 0.0).astype(jnp.bfloat16)
    return weighted[jnp.argsort(sort_order)]


def moe_routed(normed, choice_ids, gate_vals, w_g, w_u, w_d, ep_size):
    tokens, top_k = choice_ids.shape
    local_count = w_g.shape[0]
    capacity = row_capacity(tokens, top_k, ep_size)
    flat_ids = choice_ids.reshape(-1)
    dest_dev = flat_ids // local_count
    onehot_dev = (dest_dev[:, None] == jnp.arange(ep_size)[None, :]).astype(jnp.int32)
    dest_rank = jnp.sum((jnp.cumsum(onehot_dev, axis=0) - onehot_dev) * onehot_dev, axis=1)
    buf_pos = dest_dev * capacity + dest_rank
    filler = jnp.zeros((ep_size * capacity,), jnp.int32).at[buf_pos].set(jnp.arange(flat_ids.shape[0], dtype=jnp.int32) + 1)
    occupied = filler > 0
    src_slot = jnp.maximum(filler - 1, 0)
    send_rows = jnp.where(occupied[:, None], normed[src_slot // top_k], jnp.zeros((), jnp.bfloat16))
    send_gate = jnp.where(occupied, gate_vals.reshape(-1)[src_slot], 0.0)
    send_label = jnp.where(occupied, flat_ids[src_slot] % local_count, local_count).astype(jnp.float32)
    send_meta = jnp.stack([send_gate, send_label], axis=1)
    recv_rows = lax.all_to_all(send_rows, "ep", 0, 0, tiled=True)
    recv_meta = lax.all_to_all(send_meta, "ep", 0, 0, tiled=True)
    weighted = expert_rows(recv_rows, recv_meta[:, 1].astype(jnp.int32), recv_meta[:, 0], w_g, w_u, w_d)
    back_rows = lax.all_to_all(weighted, "ep", 0, 0, tiled=True)
    per_slot = back_rows[buf_pos].astype(jnp.float32).reshape(tokens, top_k, -1)
    return jnp.sum(per_slot, axis=1).astype(jnp.bfloat16)


def solution(mesh):
    ep_size = mesh.shape["ep"]
    stage_count = mesh.shape["pp"]
    rows_spec = ("dp", "ep")
    three_dim = P("pp", None, None)
    two_dim = P("pp", None)
    expert_spec = P("pp", "ep", None, None)
    cache_spec = P("pp", None, rows_spec, None, None, None)
    new_spec = P("pp", None, rows_spec, None, None)
    in_specs = (P(None, rows_spec, None), P(None, rows_spec), cache_spec, cache_spec, P("pp", None, rows_spec, None), three_dim, three_dim, three_dim, three_dim, two_dim, two_dim, three_dim, expert_spec, expert_spec, expert_spec, P(None))
    out_specs = (P(None, rows_spec, None), new_spec, new_spec)
    shift_perm = [(src_stage, src_stage + 1) for src_stage in range(stage_count - 1)]

    def device_fn(hidden_in, seq_pos, k_cache, v_cache, expert_ids, w_query, w_key, w_value, w_out, attn_gain, mlp_gain, w_router, w_gate, w_up, w_down, final_gain):
        stage_idx = lax.axis_index("pp")
        micro_count = hidden_in.shape[0]
        layer_count = w_query.shape[0]

        def run_stage(stage_in, micro_idx):
            positions = lax.dynamic_index_in_dim(seq_pos, micro_idx, 0, keepdims=False)
            hidden = stage_in
            k_list = []
            v_list = []
            for layer_idx in range(layer_count):
                k_rows = lax.dynamic_index_in_dim(k_cache[layer_idx], micro_idx, 0, keepdims=False)
                v_rows = lax.dynamic_index_in_dim(v_cache[layer_idx], micro_idx, 0, keepdims=False)
                hidden, key_new, val_new = attn_block(hidden, positions, k_rows, v_rows, w_query[layer_idx], w_key[layer_idx], w_value[layer_idx], w_out[layer_idx], attn_gain[layer_idx])
                choice_ids = lax.dynamic_index_in_dim(expert_ids[layer_idx], micro_idx, 0, keepdims=False)
                normed = rms_norm(hidden, mlp_gain[layer_idx])
                logits = jnp.dot(normed, w_router[layer_idx], preferred_element_type=jnp.float32)
                gate_vals = jax.nn.softmax(jnp.take_along_axis(logits, choice_ids, axis=1), axis=-1)
                mixed = moe_routed(normed, choice_ids, gate_vals, w_gate[layer_idx], w_up[layer_idx], w_down[layer_idx], ep_size)
                hidden = (hidden.astype(jnp.float32) + mixed.astype(jnp.float32)).astype(jnp.bfloat16)
                k_list.append(key_new)
                v_list.append(val_new)
            return hidden, jnp.stack(k_list), jnp.stack(v_list)

        def tick_step(tick_idx, loop_state):
            incoming, out_buf, k_buf, v_buf = loop_state
            micro_idx = jnp.clip(tick_idx - stage_idx, 0, micro_count - 1)
            is_valid = (tick_idx >= stage_idx) & (tick_idx - stage_idx < micro_count)
            first_in = lax.dynamic_index_in_dim(hidden_in, micro_idx, 0, keepdims=False)
            stage_in = jnp.where(stage_idx == 0, first_in, incoming)
            result, k_rows, v_rows = run_stage(stage_in, micro_idx)
            old_k = lax.dynamic_index_in_dim(k_buf, micro_idx, 1, keepdims=False)
            k_buf = lax.dynamic_update_index_in_dim(k_buf, jnp.where(is_valid, k_rows, old_k), micro_idx, 1)
            old_v = lax.dynamic_index_in_dim(v_buf, micro_idx, 1, keepdims=False)
            v_buf = lax.dynamic_update_index_in_dim(v_buf, jnp.where(is_valid, v_rows, old_v), micro_idx, 1)
            keep_out = is_valid & (stage_idx == stage_count - 1)
            old_out = lax.dynamic_index_in_dim(out_buf, micro_idx, 0, keepdims=False)
            out_buf = lax.dynamic_update_index_in_dim(out_buf, jnp.where(keep_out, result, old_out), micro_idx, 0)
            incoming = lax.ppermute(result, "pp", shift_perm)
            return incoming, out_buf, k_buf, v_buf

        new_shape = k_cache.shape[:3] + k_cache.shape[4:]
        start_state = (jnp.zeros(hidden_in.shape[1:], jnp.bfloat16), jnp.zeros(hidden_in.shape, jnp.bfloat16), jnp.zeros(new_shape, jnp.bfloat16), jnp.zeros(new_shape, jnp.bfloat16))
        end_state = lax.fori_loop(0, micro_count + stage_count - 1, tick_step, start_state)
        final_out = jnp.where(stage_idx == stage_count - 1, rms_norm(end_state[1], final_gain), jnp.zeros((), jnp.bfloat16))
        return lax.psum(final_out, "pp"), end_state[2], end_state[3]

    return jax.shard_map(device_fn, mesh=mesh, in_specs=in_specs, out_specs=out_specs, check_vma=False)
```

profile of v0, /device:TPU:0, one launch (start us, length us, event | category | flops | bytes accessed | tf_op | source)
XLA Modules:
  0.0 2445.5 jit_solution(4575093545682912409)
XLA Ops:
  12.2 2375.5 %while.22 = (s32[]{:T(128)}, bf16[16,1024]{1,0:T(8,128)(2,1)S(1)}, bf16[24,16,1024]{2,1,0:T(8,128)(2,1)}, bf16[1,24,16,8,64]{4,3,2,1,0:T(8,128)(2,1)}, bf16[1,24...) while((s32[]{:T(128)}, bf16[16,1024]{1,0:T(8,128)(2,1)S(1)}, ...), condition=%wide.region_14.15_spmd, body=%wide.region_0.14_spmd.sunk | while | flops 507501888 | bytes 47787660 | solution.py:158
  72.4 9.5 ragged-dot-none.2
  160.1 9.5 ragged-dot-none.2
  248.0 9.5 ragged-dot-none.2
  336.0 9.5 ragged-dot-none.2
  423.9 9.5 ragged-dot-none.2
  511.9 9.5 ragged-dot-none.2
  599.8 9.5 ragged-dot-none.2
  775.7 9.5 ragged-dot-none.2
  863.7 9.5 ragged-dot-none.2
  951.6 9.5 ragged-dot-none.2
  1039.6 9.5 ragged-dot-none.2
  1127.5 9.5 ragged-dot-none.2
  1215.5 9.5 ragged-dot-none.2
  1391.4 9.5 ragged-dot-none.2
  1479.4 9.5 ragged-dot-none.2
  1567.3 9.5 ragged-dot-none.2
  1655.3 9.5 ragged-dot-none.2
  1743.2 9.5 ragged-dot-none.2
  1831.2 9.5 ragged-dot-none.2
  1919.1 9.5 ragged-dot-none.2
  2007.1 9.5 ragged-dot-none.2
  2095.0 9.5 ragged-dot-none.2
  2391.5 45.1 %all-reduce.2.cloned.1.call-done = bf16[24,16,1024]{2,1,0:T(8,128)(2,1)} async-done(((bf16[24,16,1024]{2,1,0:T(8,128)(2,1)}), bf16[24,16,1024]{2,1,0:T(8,128)(2,1)}) %all-reduce.2.cloned.1.call-update) | async-done | bytes 786448 | tf_op jit(solution)/shard_map/psum | solution.py:160
  (2944 shorter events, 2166.1 us)
Async XLA Ops:
  7.2 2429.4 %all-reduce.2.cloned.1.call-start = ((), (), s32[]{:S(2)}) async-start(), calls=%async_computation.3 | async-start | bytes 1572864 | tf_op jit(solution)/shard_map/psum | solution.py:160
  36.8 13.4 all-to-all-start.1
  124.5 13.4 all-to-all-start.1
  212.4 13.4 all-to-all-start.1
  300.4 13.4 all-to-all-start.1
  388.3 13.4 all-to-all-start.1
  476.3 13.4 all-to-all-start.1
  564.2 13.4 all-to-all-start.1
  652.2 13.4 all-to-all-start.1
  740.1 13.4 all-to-all-start.1
  828.1 13.4 all-to-all-start.1
  916.0 13.4 all-to-all-start.1
  1004.0 13.4 all-to-all-start.1
  1091.9 13.4 all-to-all-start.1
  1179.9 13.4 all-to-all-start.1
  1267.9 13.4 all-to-all-start.1
  1355.8 13.4 all-to-all-start.1
  1443.8 13.4 all-to-all-start.1
  1531.7 13.4 all-to-all-start.1
  1619.7 13.4 all-to-all-start.1
  1707.6 13.4 all-to-all-start.1
  1795.6 13.4 all-to-all-start.1
  1883.5 13.4 all-to-all-start.1
  1971.5 13.4 all-to-all-start.1
  (144 other events, 3368.3 us)
Sparse Core Ops, SparseCore 0:
  2391.6 44.8 all-reduce.1
where the time goes:
time: 2480 us; the launch traced here: 2450 us
  Pallas kernels  808 us (33%)
  local copies, waits for them, and re-layouts  452 us (18%)
  other arithmetic  391 us (16%)
  starting transfers between devices  385 us (16%)
  waiting for transfers between devices  228 us (9%)
  matrix products  157 us (6%)
    another operation x81, Pallas kernels  767 us
    all_to_all x27, waiting for transfers between devices, moe_routed(): back_rows = lax.all_to_all(weighted, 'ep', 0, 0, tiled=True)  134 us
    ppermute x27, starting transfers between devices, tick_step(): incoming = lax.ppermute(result, 'pp', shift_perm)  113 us
    all_to_all x27, starting transfers between devices, moe_routed(): recv_rows = lax.all_to_all(send_rows, 'ep', 0, 0, tiled=True)  91.9 us
    all_to_all x27, starting transfers between devices, moe_routed(): back_rows = lax.all_to_all(weighted, 'ep', 0, 0, tiled=True)  91.9 us
    all_to_all x27, starting transfers between devices, moe_routed(): recv_meta = lax.all_to_all(send_meta, 'ep', 0, 0, tiled=True)  88.2 us
    sort x27, other arithmetic, expert_rows(): sort_order = jnp.argsort(labels, stable=True)  70.2 us
    sort x27, other arithmetic, expert_rows(): return weighted[jnp.argsort(sort_order)]  70.2 us
  transfers between devices with their start and end apart: 109, of which 82 were waited for; matrix products, arithmetic and copies ran while one was open for 14% of the time, Pallas kernels for 2%

commit v1 on v0

v1 whole, which is shorter than its diff:
```python
import functools

import jax
import jax.numpy as jnp
from jax import lax
from jax.experimental import pallas as pl
from jax.experimental.pallas import tpu as pltpu
from jax.sharding import PartitionSpec as P

THETA = 1000000.0
EPS = 1e-05
MICRO_PER_CHUNK = 2
MESH = pl.DeviceIdType.MESH
F32 = jnp.float32
BF16 = jnp.bfloat16


def rms(vals, gain):
    inv = lax.rsqrt(jnp.mean(vals * vals, axis=-1, keepdims=True) + EPS)
    return (vals * inv * gain).astype(BF16)


def dot(lhs, rhs):
    return jnp.dot(lhs, rhs, preferred_element_type=F32)


def dot_t(lhs, rhs):
    return lax.dot_general(lhs, rhs, (((1,), (1,)), ((), ())), preferred_element_type=F32)


def rounded(vals):
    return vals.astype(BF16).astype(F32)


def stack_kernel(cfg, hid_hbm, k_hbm, v_hbm, wq_hbm, wk_hbm, wv_hbm, wo_hbm, wg_hbm, wu_hbm, wd_hbm, cos_ref, sin_ref, tm_ref, mh_ref, ag_ref, mg_ref, fg_ref, wr_ref, out_ref, ko_ref, vo_ref, wq, wk, wv, wo, wg, wu, wd, h_in, h_mid, h_out, n_all, part, rs_sib, rs_cp, kbuf, vbuf, q2, k2, v2, o2, kn, act, coef, w_sem, kv_sem, hid_sem, ag_send, ag_recv, rs_send, rs_recv, pp_send, pp_recv, bc_send, bc_recv):
    chunks, rows, stages = cfg
    every = 4 * rows
    stage = lax.axis_index("pp")
    me = lax.axis_index("ep")
    sib = me + 1 - 2 * lax.rem(me, 2)
    cp = lax.rem(me + 2, 4)
    diag = lax.rem(sib + 2, 4)
    last = stages - 1

    def block(dev):
        return pl.ds(pl.multiple_of(dev * rows, rows), rows)

    attn_w = [pltpu.make_async_copy(src, dst, w_sem.at[i]) for i, (src, dst) in enumerate(((wq_hbm, wq), (wk_hbm, wk), (wv_hbm, wv), (wo_hbm, wo)))]
    moe_w = [pltpu.make_async_copy(src, dst, w_sem.at[i + 4]) for i, (src, dst) in enumerate(((wg_hbm, wg), (wu_hbm, wu), (wd_hbm, wd)))]

    def kv_copies(c):
        slot = lax.rem(c, 2)
        span = pl.ds(pl.multiple_of(c * rows * 128, rows * 128), rows * 128)
        return (pltpu.make_async_copy(k_hbm.at[span], kbuf.at[slot], kv_sem.at[0, slot]), pltpu.make_async_copy(v_hbm.at[span], vbuf.at[slot], kv_sem.at[1, slot]))

    hid_copy = pltpu.make_async_copy(hid_hbm, h_in, hid_sem)

    @pl.when(stage == 0)
    def _():
        hid_copy.start()

    for copy in attn_w:
        copy.start()
    for copy in kv_copies(0):
        copy.start()

    barrier = pltpu.get_barrier_semaphore()
    pl.semaphore_signal(barrier, inc=1, device_id={"ep": sib}, device_id_type=MESH)
    pl.semaphore_signal(barrier, inc=1, device_id={"ep": cp}, device_id_type=MESH)
    for step in range(1, stages):
        pl.semaphore_signal(barrier, inc=1, device_id={"pp": lax.rem(stage + step, stages)}, device_id_type=MESH)
    pl.semaphore_wait(barrier, 2 + stages - 1)

    def ag_copy(which, c):
        src = n_all.at[c, block(cp if which == 2 else me)]
        target = cp if which == 1 else sib
        return pltpu.make_async_remote_copy(src, src, ag_send.at[which, c], ag_recv.at[which, c], device_id={"ep": target}, device_id_type=MESH)

    def rs_copy(which, c):
        slot = lax.rem(c, 2)
        src = part.at[slot, block((sib, diag, cp)[which])]
        dst = rs_cp.at[c] if which == 2 else rs_sib.at[which, c]
        target = cp if which == 2 else sib
        return pltpu.make_async_remote_copy(src, dst, rs_send.at[which, c], rs_recv.at[which, c], device_id={"ep": target}, device_id_type=MESH)

    def pp_copy(c):
        return pltpu.make_async_remote_copy(h_out.at[c], h_in.at[c], pp_send.at[c], pp_recv.at[c], device_id={"pp": lax.rem(stage + 1, stages)}, device_id_type=MESH)

    def bc_copy(c, target):
        return pltpu.make_async_remote_copy(out_ref.at[c], out_ref.at[c], bc_send.at[target, c], bc_recv.at[c], device_id={"pp": target}, device_id_type=MESH)

    lane = lax.broadcasted_iota(jnp.int32, (rows, 128), 1)
    low_half = lane < 64
    first_part = lax.rem(lane, 64) < 32
    own_head = lax.rem(lax.broadcasted_iota(jnp.int32, (16, 128), 1), 8) == lax.broadcasted_iota(jnp.int32, (16, 128), 0) // 2

    def rope(vals, cos, sin):
        turned = jnp.where(first_part, pltpu.roll(vals, 96, 1), pltpu.roll(vals, 32, 1))
        return rounded(vals * cos + turned * sin)

    def attend(c):
        slot = lax.rem(c, 2)

        @pl.when(stage > 0)
        def _():
            pp_copy(c).wait_recv()

        @pl.when((stage == 0) & (c == 0))
        def _():
            hid_copy.wait()

        @pl.when(c == 0)
        def _():
            for copy in attn_w:
                copy.wait()
            for copy in moe_w:
                copy.start()

        @pl.when(c + 1 < chunks)
        def _():
            for copy in kv_copies(c + 1):
                copy.start()

        span = pl.ds(pl.multiple_of(c * rows, rows), rows)
        cos = cos_ref[span, :]
        sin = sin_ref[span, :]
        hidden = h_in[c].astype(F32)
        normed = rms(hidden, ag_ref[...])
        query = rounded(dot(normed, wq[...]))
        key = rounded(dot(normed, wk[...]))
        value = rounded(dot(normed, wv[...]))
        for j in range(8):
            piece = rope(query[:, j * 128:(j + 1) * 128], cos, sin)
            q2[pl.ds(2 * j, rows, stride=16), :] = piece
            q2[pl.ds(2 * j + 1, rows, stride=16), :] = pltpu.roll(piece, 64, 1)
        for which, full in ((0, key), (1, value)):
            spread = (k2, v2)[which]
            for j in range(4):
                piece = full[:, j * 128:(j + 1) * 128]
                if which == 0:
                    piece = rope(piece, cos, sin)
                other = pltpu.roll(piece, 64, 1)
                kn[which, pl.ds(2 * j, rows, stride=8), :] = piece
                kn[which, pl.ds(2 * j + 1, rows, stride=8), :] = other
                spread[pl.ds(4 * j, rows, stride=16), :] = piece
                spread[pl.ds(4 * j + 1, rows, stride=16), :] = piece
                spread[pl.ds(4 * j + 2, rows, stride=16), :] = other
                spread[pl.ds(4 * j + 3, rows, stride=16), :] = other
        new_span = pl.ds(pl.multiple_of(c * rows * 8, rows * 8), rows * 8)
        ko_ref[new_span, :] = kn[0, :, :64].astype(BF16)
        vo_ref[new_span, :] = kn[1, :, :64].astype(BF16)
        for copy in kv_copies(c):
            copy.wait()

        @pl.loop(0, rows // 8)
        def _(g):
            heads = pl.ds(pl.multiple_of(g * 128, 128), 128)
            q_f32 = q2[heads, :64]
            q_bf = q_f32.astype(BF16)
            scores = []
            for b in range(8):
                keys = kbuf[slot, pl.ds(pl.multiple_of((g * 8 + b) * 128, 128), 128), :]
                valid = tm_ref[pl.ds(c * rows + g * 8 + b, 1), :] > 0
                one = dot_t(q_bf[b * 16:(b + 1) * 16], keys) * 0.125
                scores.append(jnp.where(own_head & valid, one, -jnp.inf))
            score = jnp.concatenate(scores, axis=0)
            self_score = jnp.sum(q_f32 * k2[heads, :64], axis=1, keepdims=True) * 0.125
            top = jnp.maximum(jnp.max(score, axis=1, keepdims=True), self_score)
            weight = jnp.exp(score - top)
            self_w = jnp.exp(self_score - top)
            total = jnp.sum(weight, axis=1, keepdims=True) + self_w
            weight = (weight / total).astype(BF16)
            self_w = rounded(self_w / total)
            outs = []
            for b in range(8):
                vals = vbuf[slot, pl.ds(pl.multiple_of((g * 8 + b) * 128, 128), 128), :]
                outs.append(dot(weight[b * 16:(b + 1) * 16], vals))
            mixed = jnp.concatenate(outs, axis=0) + self_w * v2[heads, :64]
            o2[heads, :64] = mixed

        pieces = []
        for j in range(8):
            even = o2[pl.ds(2 * j, rows, stride=16), :]
            odd = o2[pl.ds(2 * j + 1, rows, stride=16), :]
            pieces.append(jnp.where(low_half, even, pltpu.roll(odd, 64, 1)).astype(BF16))
        attn_out = jnp.concatenate(pieces, axis=1)
        mid = (hidden + dot(attn_out, wo[...])).astype(BF16)
        h_mid[c] = mid
        n_all[c, block(me), :] = rms(mid.astype(F32), mg_ref[...])
        ag_copy(1, c).start()
        ag_copy(0, c).start()

    def gates(c):
        logits = dot_t(n_all[c], wr_ref[...])
        chosen = mh_ref[pl.ds(pl.multiple_of(c * every, every), every), :] > 0
        logits = jnp.where(chosen, logits, -jnp.inf)
        grown = jnp.exp(logits - jnp.max(logits, axis=1, keepdims=True))
        coef[...] = grown / jnp.sum(grown, axis=1, keepdims=True)

    def experts(c, first, count):
        slot = lax.rem(c, 2)
        expert_lane = lax.broadcasted_iota(jnp.int32, (every, 32), 1)

        @pl.loop(first, first + count)
        def _(j):
            for f in range(2):
                cols = slice(f * 256, (f + 1) * 256)
                gate_h = dot(n_all[c], wg[j, :, cols])
                up_h = dot(n_all[c], wu[j, :, cols])
                act[:, cols] = (gate_h / (1.0 + jnp.exp(-gate_h)) * up_h).astype(BF16)
            col = jnp.sum(jnp.where(expert_lane == me * 8 + j, coef[...], 0.0), axis=1, keepdims=True)
            for f in range(4):
                cols = slice(f * 256, (f + 1) * 256)
                down = dot(act[...], wd[j, :, cols])
                part[slot, :, cols] += rounded(col * down)

    @pl.loop(0, chunks + 2)
    def _(i):
        @pl.when(i < chunks)
        def _():
            attend(i)

        @pl.when(i >= 2)
        def _():
            c = i - 2
            slot = lax.rem(c, 2)
            rs_copy(0, c).wait_recv()
            rs_copy(1, c).wait_recv()
            part[slot, block(cp), :] += rs_sib[1, c]
            rs_copy(2, c).start()

        has_moe = (i >= 1) & (i <= chunks)

        @pl.when(has_moe)
        def _():
            c = i - 1

            @pl.when(c == 0)
            def _():
                for copy in moe_w:
                    copy.wait()

            @pl.when(c >= 2)
            def _():
                for which in range(3):
                    rs_copy(which, c - 2).wait_send()

            part[lax.rem(c, 2)] = jnp.zeros((every, part.shape[2]), F32)
            ag_copy(0, c).wait_recv()
            ag_copy(2, c).wait_recv()
            gates(c)
            experts(c, 0, 4)

        @pl.when(i < chunks)
        def _():
            ag_copy(1, i).wait_recv()
            ag_copy(2, i).start()

        @pl.when(has_moe)
        def _():
            c = i - 1
            experts(c, 4, 4)
            rs_copy(1, c).start()
            rs_copy(0, c).start()

        @pl.when(i >= 2)
        def _():
            c = i - 2
            slot = lax.rem(c, 2)
            rs_copy(2, c).wait_recv()
            total = part[slot, block(me), :] + rs_sib[0, c] + rs_cp[c]
            result = (h_mid[c].astype(F32) + rounded(total)).astype(BF16)

            @pl.when(stage < last)
            def _():
                h_out[c] = result
                pp_copy(c).start()

            @pl.when(stage == last)
            def _():
                out_ref[c] = rms(result.astype(F32), fg_ref[...])
                for target in range(last):
                    bc_copy(c, target).start()

    for which in range(3):
        rs_copy(which, chunks - 2).wait_send()
        rs_copy(which, chunks - 1).wait_send()

    @pl.loop(0, chunks)
    def _(c):
        for which in range(3):
            ag_copy(which, c).wait_send()

        @pl.when(stage < last)
        def _():
            pp_copy(c).wait_send()
            bc_copy(c, 0).wait_recv()

        @pl.when(stage == last)
        def _():
            for target in range(last):
                bc_copy(c, target).wait_send()


def run_stack(cfg, hidden, k_rows, v_rows, weights, cos, sin, time_mask, multi_hot, gains, router):
    chunks, rows, stages = cfg
    every = 4 * rows
    width = hidden.shape[-1]
    w_q, w_k, w_v, w_o, w_g, w_u, w_d = weights
    vmem = pl.BlockSpec(memory_space=pltpu.VMEM)
    hbm = pl.BlockSpec(memory_space=pl.ANY)
    dma = pltpu.SemaphoreType.DMA
    new_shape = jax.ShapeDtypeStruct((chunks * rows * 8, 64), BF16)
    return pl.pallas_call(
        functools.partial(stack_kernel, cfg),
        out_shape=(jax.ShapeDtypeStruct((chunks, rows, width), BF16), new_shape, new_shape),
        in_specs=[hbm] * 10 + [vmem] * 8,
        out_specs=(vmem, vmem, vmem),
        scratch_shapes=[
            pltpu.VMEM(w_q.shape, BF16),
            pltpu.VMEM(w_k.shape, BF16),
            pltpu.VMEM(w_v.shape, BF16),
            pltpu.VMEM(w_o.shape, BF16),
            pltpu.VMEM(w_g.shape, BF16),
            pltpu.VMEM(w_u.shape, BF16),
            pltpu.VMEM(w_d.shape, BF16),
            pltpu.VMEM((chunks, rows, width), BF16),
            pltpu.VMEM((chunks, rows, width), BF16),
            pltpu.VMEM((chunks, rows, width), BF16),
            pltpu.VMEM((chunks, every, width), BF16),
            pltpu.VMEM((2, every, width), F32),
            pltpu.VMEM((2, chunks, rows, width), F32),
            pltpu.VMEM((chunks, rows, width), F32),
            pltpu.VMEM((2, rows * 128, 64), BF16),
            pltpu.VMEM((2, rows * 128, 64), BF16),
            pltpu.VMEM((rows * 16, 128), F32),
            pltpu.VMEM((rows * 16, 128), F32),
            pltpu.VMEM((rows * 16, 128), F32),
            pltpu.VMEM((rows * 16, 128), F32),
            pltpu.VMEM((2, rows * 8, 128), F32),
            pltpu.VMEM((every, w_g.shape[2]), BF16),
            pltpu.VMEM((every, 32), F32),
            dma((7,)),
            dma((2, 2)),
            dma,
            dma((3, chunks)),
            dma((3, chunks)),
            dma((3, chunks)),
            dma((3, chunks)),
            dma((chunks,)),
            dma((chunks,)),
            dma((3, chunks)),
            dma((chunks,)),
        ],
        compiler_params=pltpu.CompilerParams(collective_id=0, has_side_effects=True, vmem_limit_bytes=67043328),
    )(hidden, k_rows, v_rows, w_q, w_k, w_v, w_o, w_g, w_u, w_d, cos, sin, time_mask, multi_hot, *gains, router)


def solution(mesh):
    stages = mesh.shape["pp"]
    rows_spec = ("dp", "ep")
    three_dim = P("pp", None, None)
    two_dim = P("pp", None)
    expert_spec = P("pp", "ep", None, None)
    cache_spec = P("pp", None, rows_spec, None, None, None)
    new_spec = P("pp", None, rows_spec, None, None)
    in_specs = (P(None, rows_spec, None), P(None, rows_spec), cache_spec, cache_spec, P("pp", None, rows_spec, None), three_dim, three_dim, three_dim, three_dim, two_dim, two_dim, three_dim, expert_spec, expert_spec, expert_spec, P(None))
    out_specs = (P(None, rows_spec, None), new_spec, new_spec)

    def device_fn(hidden_in, seq_pos, k_cache, v_cache, expert_ids, w_query, w_key, w_value, w_out, attn_gain, mlp_gain, w_router, w_gate, w_up, w_down, final_gain):
        micro, tokens, width = hidden_in.shape
        rows = MICRO_PER_CHUNK * tokens
        chunks = micro // MICRO_PER_CHUNK
        pos = seq_pos.reshape(micro * tokens, 1)
        lanes = jnp.arange(128)
        half = 32
        inv_freq = THETA ** (-jnp.arange(half, dtype=F32) / half)
        angles = pos.astype(F32) * jnp.tile(inv_freq, 4)[None, :]
        cos = jnp.cos(angles)
        sin = jnp.where(lanes % 64 < 32, -1.0, 1.0) * jnp.sin(angles)
        time_mask = (lanes[None, :] // 8 < pos).astype(F32)
        ids = lax.all_gather(expert_ids[0], "ep", axis=0)
        ids = ids.reshape(4, chunks, rows, 8).transpose(1, 0, 2, 3).reshape(chunks * 4 * rows, 8)
        multi_hot = jnp.sum((ids[:, :, None] == jnp.arange(32)[None, None, :]).astype(F32), axis=1)
        gains = (attn_gain.astype(F32), mlp_gain.astype(F32), final_gain.astype(F32).reshape(1, width))
        weights = (w_query[0], w_key[0], w_value[0], w_out[0], w_gate[0], w_up[0], w_down[0])
        out, k_new, v_new = run_stack((chunks, rows, stages), hidden_in.reshape(chunks, rows, width), k_cache.reshape(-1, 64), v_cache.reshape(-1, 64), weights, cos, sin, time_mask, multi_hot, gains, w_router[0].T)
        new_shape = k_cache.shape[:3] + k_cache.shape[4:]
        return out.reshape(hidden_in.shape), k_new.reshape(new_shape), v_new.reshape(new_shape)

    return jax.shard_map(device_fn, mesh=mesh, in_specs=in_specs, out_specs=out_specs, check_vma=False)
```

time: 2480 us -> 268 us (0.11); the launches traced: 2450 us -> 268 us
  Pallas kernels: 808 us -> 245 us
  local copies, waits for them, and re-layouts: 452 us -> 8.96 us
  starting transfers between devices: 385 us -> 0 us
  other arithmetic: 391 us -> 6.3 us
  waiting for transfers between devices: 228 us -> 0 us
  matrix products: 157 us -> 0 us
    another operation x81 -> x0, Pallas kernels: 767 us -> none
    gather x351 -> x0, local copies, waits for them, and re-layouts: 306 us -> none  [the longest x135 42.9 us: run_stage(): jnp.take_along_axis(logits, choice_ids, axis=1)]
    all_to_all x81 -> x0, starting transfers between devices: 272 us -> none  [the longest x27 91.9 us: moe_routed(): recv_rows = lax.all_to_all(send_rows, 'ep', 0, 0, tiled=True)]
    pallas_call x0 -> x1, Pallas kernels: none -> 245 us  [run_stack(): pl.pallas_call(functools.partial(stack_kernel, cfg), out_shape=(jax.Shape...]
    all_to_all x81 -> x0, waiting for transfers between devices: 180 us -> none  [the longest x27 134 us: moe_routed(): back_rows = lax.all_to_all(weighted, 'ep', 0, 0, tiled=True)]
    dot_general x216 -> x0, matrix products: 157 us -> none  [the longest x27 56.5 us: attn_block(): jnp.dot(attn_out, w_o, preferred_element_type=jnp.float32)]
    sort x54 -> x0, other arithmetic: 140 us -> none  [the longest x27 70.2 us: expert_rows(): sort_order = jnp.argsort(labels, stable=True)]
    ppermute x27 -> x0, starting transfers between devices: 113 us -> none  [tick_step(): incoming = lax.ppermute(result, 'pp', shift_perm)]
  transfers between devices with their start and end apart: 109 -> 0, of which waited for: 82 -> 0; matrix products, arithmetic and copies ran while one was open for 14% -> 0% of each run, Pallas kernels for 2% -> 0%
where the time goes in v1:
time: 268 us
  Pallas kernels  245 us (91%)
  local copies, waits for them, and re-layouts  8.96 us (3%)
  blocking collectives  7.27 us (3%)
  other arithmetic  6.3 us (2%)
    pallas_call x1, Pallas kernels, run_stack(): pl.pallas_call(functools.partial(stack_kernel, cfg), out_shape=(jax.Shape...  245 us
    all_gather x1, blocking collectives, device_fn(): ids = lax.all_gather(expert_ids[0], 'ep', axis=0)  7.27 us
    unnamed x4, local copies, waits for them, and re-layouts  7.03 us

profile of v1, /device:TPU:0, one launch (start us, length us, event | category | flops | bytes accessed | tf_op | source)
XLA Modules:
  0.0 267.8 jit_solution(6076032745519091015)
XLA Ops:
  0.7 0.1 mul.24
  0.8 1.3 convert_element_type.24.ag_ref
  2.0 1.3 convert_element_type.25.mg_ref
  3.3 1.3 reshape.109
  4.6 0.8 copy.27
  5.3 0.1 reshape.102
  5.4 0.8 compare_convert_fusion.tm_ref
  6.2 7.3 %all_gather.3 = s32[4,24,16,8]{1,3,2,0:T(8,128)S(1)} all-gather(s32[1,24,16,8]{1,3,2,0:T(8,128)} %param.20), channel_id=1, replica_groups=mesh['dp'=2,'pp'=4,'ep'=4] {'ep'}, dimensions={0}, use_global_device_ids=true | all-gather | bytes 61440 | tf_op jit(solution)/shard_map/all_gather | solution.py:382
  13.5 0.2 copy.28
  13.7 0.1 reshape.103
  13.8 0.1 copy.29
  13.9 0.2 eq.17
  14.1 0.2 convert_reduce_fusion
  14.3 1.5 fusion
  15.8 1.2 copy.30.mh_ref
  16.9 244.6 %shard_map.175 = (bf16[12,32,1024]{2,1,0:T(8,128)(2,1)}, bf16[3072,64]{1,0:T(8,128)(2,1)}, bf16[3072,64]{1,0:T(8,128)(2,1)}) custom-call(bf16[12,32,1024]{2,1,0:T(8,128)(2,1)} %bitcast.34, bf16[49152,64]{1,0:T(8,128)(2,1)} %bitcast.24, bf16[49152,64]{1,0:T(8,128)(2,1)} %bitcast.25, bf16[1024,1024]{1,0:T(8,128)(2,1)} %bitcast.29, bf16[1024,512]{1,0:T(8,128)(2,1)} %bitcast.31, ...), custom_call_target="tpu_custom_call" | custom-call | tf_op jit(solution)/shard_map/pallas_call | solution.py:314
  261.5 2.1 copy.34
  263.6 2.1 copy.35
  265.7 2.1 copy.36
  (5 shorter events, 0.0 us)

commit v2 on v1

--- a/solution.py
+++ b/solution.py
@@ -2,6 +2,7 @@
 
 import jax
 import jax.numpy as jnp
+import numpy as np
 from jax import lax
 from jax.experimental import pallas as pl
 from jax.experimental.pallas import tpu as pltpu
@@ -10,6 +11,7 @@
 THETA = 1000000.0
 EPS = 1e-05
 MICRO_PER_CHUNK = 2
+UNROLL = 4
 MESH = pl.DeviceIdType.MESH
 F32 = jnp.float32
 BF16 = jnp.bfloat16
@@ -17,7 +19,7 @@
 
 def rms(vals, gain):
     inv = lax.rsqrt(jnp.mean(vals * vals, axis=-1, keepdims=True) + EPS)
-    return (vals * inv * gain).astype(BF16)
+    return (vals * inv * gain.astype(F32)).astype(BF16)
 
 
 def dot(lhs, rhs):
@@ -32,7 +34,7 @@
     return vals.astype(BF16).astype(F32)
 
 
-def stack_kernel(cfg, hid_hbm, k_hbm, v_hbm, wq_hbm, wk_hbm, wv_hbm, wo_hbm, wg_hbm, wu_hbm, wd_hbm, cos_ref, sin_ref, tm_ref, mh_ref, ag_ref, mg_ref, fg_ref, wr_ref, out_ref, ko_ref, vo_ref, wq, wk, wv, wo, wg, wu, wd, h_in, h_mid, h_out, n_all, part, rs_sib, rs_cp, kbuf, vbuf, q2, k2, v2, o2, kn, act, coef, w_sem, kv_sem, hid_sem, ag_send, ag_recv, rs_send, rs_recv, pp_send, pp_recv, bc_send, bc_recv):
+def stack_kernel(cfg, hid_hbm, k_hbm, v_hbm, wq_hbm, wk_hbm, wv_hbm, wo_hbm, wg_hbm, wu_hbm, wd_hbm, rot_ref, pos_ref, ids_ref, ag_ref, mg_ref, fg_ref, wr_ref, out_ref, ko_ref, vo_ref, wq, wk, wv, wo, wg, wu, wd, h_in, h_mid, h_out, n_all, part, rs_sib, rs_cp, kbuf, vbuf, q2, k2, v2, o2, kn, act_even, act_odd, coef, pos_col, bits, w_sem, kv_sem, hid_sem, bit_send, bit_recv, ag_send, ag_recv, rs_send, rs_recv, pp_send, pp_recv, bc_send, bc_recv):
     chunks, rows, stages = cfg
     every = 4 * rows
     stage = lax.axis_index("pp")
@@ -46,7 +48,8 @@
         return pl.ds(pl.multiple_of(dev * rows, rows), rows)
 
     attn_w = [pltpu.make_async_copy(src, dst, w_sem.at[i]) for i, (src, dst) in enumerate(((wq_hbm, wq), (wk_hbm, wk), (wv_hbm, wv), (wo_hbm, wo)))]
-    moe_w = [pltpu.make_async_copy(src, dst, w_sem.at[i + 4]) for i, (src, dst) in enumerate(((wg_hbm, wg), (wu_hbm, wu), (wd_hbm, wd)))]
+    def expert_w(j):
+        return [pltpu.make_async_copy(src.at[j], dst.at[j], w_sem.at[4 + which * 8 + j]) for which, (src, dst) in enumerate(((wg_hbm, wg), (wu_hbm, wu), (wd_hbm, wd)))]
 
     def kv_copies(c):
         slot = lax.rem(c, 2)
@@ -67,9 +70,23 @@
     barrier = pltpu.get_barrier_semaphore()
     pl.semaphore_signal(barrier, inc=1, device_id={"ep": sib}, device_id_type=MESH)
     pl.semaphore_signal(barrier, inc=1, device_id={"ep": cp}, device_id_type=MESH)
+    pl.semaphore_signal(barrier, inc=1, device_id={"ep": diag}, device_id_type=MESH)
     for step in range(1, stages):
         pl.semaphore_signal(barrier, inc=1, device_id={"pp": lax.rem(stage + step, stages)}, device_id_type=MESH)
-    pl.semaphore_wait(barrier, 2 + stages - 1)
+
+    marks = jnp.zeros((16, ids_ref.shape[2]), jnp.int32)
+    for k in range(8):
+        marks = marks | lax.shift_left(jnp.int32(1), ids_ref[:, k, :])
+    micro = marks.shape[1]
+    bits[me, 0, :, :micro] = (marks & 65535).astype(F32)
+    bits[me, 1, :, :micro] = (lax.shift_right_logical(marks, jnp.int32(16)) & 65535).astype(F32)
+    pl.semaphore_wait(barrier, 3 + stages - 1)
+
+    def bit_copy(which):
+        return pltpu.make_async_remote_copy(bits.at[me], bits.at[me], bit_send.at[which], bit_recv.at[which], device_id={"ep": (sib, cp, diag)[which]}, device_id_type=MESH)
+
+    for which in range(3):
+        bit_copy(which).start()
 
     def ag_copy(which, c):
         src = n_all.at[c, block(cp if which == 2 else me)]
@@ -94,12 +111,13 @@
     first_part = lax.rem(lane, 64) < 32
     own_head = lax.rem(lax.broadcasted_iota(jnp.int32, (16, 128), 1), 8) == lax.broadcasted_iota(jnp.int32, (16, 128), 0) // 2
 
+    slot_of_lane = (lax.broadcasted_iota(jnp.int32, (1, 128), 1) // 8).astype(F32)
+
     def rope(vals, cos, sin):
         turned = jnp.where(first_part, pltpu.roll(vals, 96, 1), pltpu.roll(vals, 32, 1))
         return rounded(vals * cos + turned * sin)
 
-    def attend(c):
-        slot = lax.rem(c, 2)
+    def project(c):
 
         @pl.when(stage > 0)
         def _():
@@ -113,19 +131,29 @@
         def _():
             for copy in attn_w:
                 copy.wait()
-            for copy in moe_w:
-                copy.start()
+
+            @pl.loop(0, 8)
+            def _(j):
+                for copy in expert_w(j):
+                    copy.start()
 
         @pl.when(c + 1 < chunks)
         def _():
             for copy in kv_copies(c + 1):
                 copy.start()
 
-        span = pl.ds(pl.multiple_of(c * rows, rows), rows)
-        cos = cos_ref[span, :]
-        sin = sin_ref[span, :]
-        hidden = h_in[c].astype(F32)
-        normed = rms(hidden, ag_ref[...])
+        for m in range(rows // 16):
+            at = lax.broadcasted_iota(jnp.int32, pos_ref.shape, 1) == c * (rows // 16) + m
+            col = jnp.sum(jnp.where(at, pos_ref[...], 0).astype(F32), axis=1, keepdims=True)
+            pos_col[m * 16:(m + 1) * 16, :] = jnp.broadcast_to(col, (16, 128))
+        where_pos = pos_col[...]
+        cos = jnp.zeros((rows, 128), F32)
+        sin = jnp.zeros((rows, 128), F32)
+        for p in range(16):
+            here = where_pos == p + 1.0
+            cos = jnp.where(here, rot_ref[0, p:p + 1, :], cos)
+            sin = jnp.where(here, rot_ref[1, p:p + 1, :], sin)
+        normed = rms(h_in[c].astype(F32), ag_ref[...])
         query = rounded(dot(normed, wq[...]))
         key = rounded(dot(normed, wk[...]))
         value = rounded(dot(normed, wv[...]))
@@ -149,10 +177,13 @@
         new_span = pl.ds(pl.multiple_of(c * rows * 8, rows * 8), rows * 8)
         ko_ref[new_span, :] = kn[0, :, :64].astype(BF16)
         vo_ref[new_span, :] = kn[1, :, :64].astype(BF16)
+
+    def attend(c):
+        slot = lax.rem(c, 2)
         for copy in kv_copies(c):
             copy.wait()
 
-        @pl.loop(0, rows // 8)
+        @pl.loop(0, rows // 8, unroll=UNROLL)
         def _(g):
             heads = pl.ds(pl.multiple_of(g * 128, 128), 128)
             q_f32 = q2[heads, :64]
@@ -160,7 +191,7 @@
             scores = []
             for b in range(8):
                 keys = kbuf[slot, pl.ds(pl.multiple_of((g * 8 + b) * 128, 128), 128), :]
-                valid = tm_ref[pl.ds(c * rows + g * 8 + b, 1), :] > 0
+                valid = pos_col[pl.ds(g * 8 + b, 1), :] > slot_of_lane
                 one = dot_t(q_bf[b * 16:(b + 1) * 16], keys) * 0.125
                 scores.append(jnp.where(own_head & valid, one, -jnp.inf))
             score = jnp.concatenate(scores, axis=0)
@@ -184,7 +215,7 @@
             odd = o2[pl.ds(2 * j + 1, rows, stride=16), :]
             pieces.append(jnp.where(low_half, even, pltpu.roll(odd, 64, 1)).astype(BF16))
         attn_out = jnp.concatenate(pieces, axis=1)
-        mid = (hidden + dot(attn_out, wo[...])).astype(BF16)
+        mid = (h_in[c].astype(F32) + dot(attn_out, wo[...])).astype(BF16)
         h_mid[c] = mid
         n_all[c, block(me), :] = rms(mid.astype(F32), mg_ref[...])
         ag_copy(1, c).start()
@@ -192,44 +223,100 @@
 
     def gates(c):
         logits = dot_t(n_all[c], wr_ref[...])
-        chosen = mh_ref[pl.ds(pl.multiple_of(c * every, every), every), :] > 0
+        lane32 = lax.broadcasted_iota(jnp.int32, (16, 32), 1)
+        flags = []
+        for src in range(4):
+            for m in range(rows // 16):
+                at = lax.broadcasted_iota(jnp.int32, (16, 128), 1) == c * (rows // 16) + m
+                low = jnp.sum(jnp.where(at, bits[src, 0], 0.0), axis=1, keepdims=True)
+                high = jnp.sum(jnp.where(at, bits[src, 1], 0.0), axis=1, keepdims=True)
+                halves = jnp.where(lane32 < 16, low, high).astype(jnp.int32)
+                flags.append(lax.shift_right_logical(halves, lax.rem(lane32, 16)) & 1)
+        chosen = jnp.concatenate(flags, axis=0) > 0
         logits = jnp.where(chosen, logits, -jnp.inf)
         grown = jnp.exp(logits - jnp.max(logits, axis=1, keepdims=True))
-        coef[...] = grown / jnp.sum(grown, axis=1, keepdims=True)
-
-    def experts(c, first, count):
-        slot = lax.rem(c, 2)
+        share = grown / jnp.sum(grown, axis=1, keepdims=True)
         expert_lane = lax.broadcasted_iota(jnp.int32, (every, 32), 1)
-
+        for j in range(8):
+            col = jnp.sum(jnp.where(expert_lane == me * 8 + j, share, 0.0), axis=1, keepdims=True)
+            coef[j] = jnp.broadcast_to(col, (every, 128))
+
+    def gate_up(c, j, act):
+        for f in range(2):
+            here = slice(f * 256, (f + 1) * 256)
+            gate_h = dot(n_all[c], wg[j, :, here])
+            up_h = dot(n_all[c], wu[j, :, here])
+            act[:, here] = (gate_h / (1.0 + jnp.exp(-gate_h)) * up_h).astype(BF16)
+
+    def down(c, j, act):
+        slot = lax.rem(c, 2)
+        scale = coef[j]
+        for f in range(4):
+            term = dot(act[...], wd[j, :, f * 256:(f + 1) * 256])
+            for v in range(2):
+                here = slice(f * 256 + v * 128, f * 256 + (v + 1) * 128)
+                part[slot, :, here] += rounded(scale * term[:, v * 128:(v + 1) * 128])
+
+    def expert_pairs(c, first, count):
         @pl.loop(first, first + count)
+        def _(t):
+            gate_up(c, 2 * t + 1, act_odd)
+            down(c, 2 * t, act_even)
+            gate_up(c, 2 * t + 2, act_even)
+            down(c, 2 * t + 1, act_odd)
+
+    def loading_experts(c):
+        @pl.loop(0, 8)
         def _(j):
-            for f in range(2):
-                cols = slice(f * 256, (f + 1) * 256)
-                gate_h = dot(n_all[c], wg[j, :, cols])
-                up_h = dot(n_all[c], wu[j, :, cols])
-                act[:, cols] = (gate_h / (1.0 + jnp.exp(-gate_h)) * up_h).astype(BF16)
-            col = jnp.sum(jnp.where(expert_lane == me * 8 + j, coef[...], 0.0), axis=1, keepdims=True)
-            for f in range(4):
-                cols = slice(f * 256, (f + 1) * 256)
-                down = dot(act[...], wd[j, :, cols])
-                part[slot, :, cols] += rounded(col * down)
+            for copy in expert_w(j):
+                copy.wait()
+            gate_up(c, j, act_even)
+            down(c, j, act_even)
+
+    def chip_sum(c):
+        slot = lax.rem(c, 2)
+        rs_copy(0, c).wait_recv()
+        rs_copy(1, c).wait_recv()
+        part[slot, block(cp), :] += rs_sib[1, c]
+        rs_copy(2, c).start()
+
+    def finish(c):
+        slot = lax.rem(c, 2)
+        rs_copy(2, c).wait_recv()
+        total = part[slot, block(me), :] + rs_sib[0, c] + rs_cp[c]
+        result = (h_mid[c].astype(F32) + rounded(total)).astype(BF16)
+
+        @pl.when(stage < last)
+        def _():
+            h_out[c] = result
+            pp_copy(c).start()
+
+        @pl.when(stage == last)
+        def _():
+            out_ref[c] = rms(result.astype(F32), fg_ref[...].astype(F32).reshape(1, -1))
+            for target in range(last):
+                bc_copy(c, target).start()
 
     @pl.loop(0, chunks + 2)
     def _(i):
         @pl.when(i < chunks)
         def _():
+            project(i)
+
+        @pl.when(i >= 2)
+        def _():
+            chip_sum(i - 2)
+
+        has_moe = (i >= 1) & (i <= chunks)
+
+        @pl.when(has_moe)
+        def _():
+            ag_copy(1, i - 1).wait_recv()
+            ag_copy(2, i - 1).start()
+
+        @pl.when(i < chunks)
+        def _():
             attend(i)
-
-        @pl.when(i >= 2)
-        def _():
-            c = i - 2
-            slot = lax.rem(c, 2)
-            rs_copy(0, c).wait_recv()
-            rs_copy(1, c).wait_recv()
-            part[slot, block(cp), :] += rs_sib[1, c]
-            rs_copy(2, c).start()
-
-        has_moe = (i >= 1) & (i <= chunks)
 
         @pl.when(has_moe)
         def _():
@@ -237,8 +324,8 @@
 
             @pl.when(c == 0)
             def _():
-                for copy in moe_w:
-                    copy.wait()
+                for which in range(3):
+                    bit_copy(which).wait_recv()
 
             @pl.when(c >= 2)
             def _():
@@ -249,40 +336,36 @@
             ag_copy(0, c).wait_recv()
             ag_copy(2, c).wait_recv()
             gates(c)
-            experts(c, 0, 4)
-
-        @pl.when(i < chunks)
-        def _():
-            ag_copy(1, i).wait_recv()
-            ag_copy(2, i).start()
+
+            @pl.when(c == 0)
+            def _():
+                loading_experts(c)
+
+            @pl.when(c > 0)
+            def _():
+                gate_up(c, 0, act_even)
+                expert_pairs(c, 0, 2)
+
+        @pl.when(i >= 2)
+        def _():
+            finish(i - 2)
 
         @pl.when(has_moe)
         def _():
             c = i - 1
-            experts(c, 4, 4)
+
+            @pl.when(c > 0)
+            def _():
+                expert_pairs(c, 2, 1)
+                gate_up(c, 7, act_odd)
+                down(c, 6, act_even)
+                down(c, 7, act_odd)
+
             rs_copy(1, c).start()
             rs_copy(0, c).start()
 
-        @pl.when(i >= 2)
-        def _():
-            c = i - 2
-            slot = lax.rem(c, 2)
-            rs_copy(2, c).wait_recv()
-            total = part[slot, block(me), :] + rs_sib[0, c] + rs_cp[c]
-            result = (h_mid[c].astype(F32) + rounded(total)).astype(BF16)
-
-            @pl.when(stage < last)
-            def _():
-                h_out[c] = result
-                pp_copy(c).start()
-
-            @pl.when(stage == last)
-            def _():
-                out_ref[c] = rms(result.astype(F32), fg_ref[...])
-                for target in range(last):
-                    bc_copy(c, target).start()
-
     for which in range(3):
+        bit_copy(which).wait_send()
         rs_copy(which, chunks - 2).wait_send()
         rs_copy(which, chunks - 1).wait_send()
 
@@ -302,7 +385,25 @@
                 bc_copy(c, target).wait_send()
 
 
-def run_stack(cfg, hidden, k_rows, v_rows, weights, cos, sin, time_mask, multi_hot, gains, router):
+def place_kernel(a_ref, b_ref, c_ref, a_out, b_out, c_out, sems):
+    copies = [pltpu.make_async_copy(src, dst, sems.at[i]) for i, (src, dst) in enumerate(((a_ref, a_out), (b_ref, b_out), (c_ref, c_out)))]
+    for copy in copies:
+        copy.start()
+    for copy in copies:
+        copy.wait()
+
+
+def place(arrays):
+    return pl.pallas_call(
+        place_kernel,
+        out_shape=tuple(jax.ShapeDtypeStruct(arr.shape, arr.dtype) for arr in arrays),
+        in_specs=[pl.BlockSpec(memory_space=pltpu.VMEM)] * 3,
+        out_specs=(pl.BlockSpec(memory_space=pl.ANY),) * 3,
+        scratch_shapes=[pltpu.SemaphoreType.DMA((3,))],
+    )(*arrays)
+
+
+def run_stack(cfg, hidden, k_rows, v_rows, weights, rotation, positions, ids, gains, router):
     chunks, rows, stages = cfg
     every = 4 * rows
     width = hidden.shape[-1]
@@ -314,7 +415,7 @@
     return pl.pallas_call(
         functools.partial(stack_kernel, cfg),
         out_shape=(jax.ShapeDtypeStruct((chunks, rows, width), BF16), new_shape, new_shape),
-        in_specs=[hbm] * 10 + [vmem] * 8,
+        in_specs=[hbm] * 10 + [vmem] * 7,
         out_specs=(vmem, vmem, vmem),
         scratch_shapes=[
             pltpu.VMEM(w_q.shape, BF16),
@@ -339,10 +440,15 @@
             pltpu.VMEM((rows * 16, 128), F32),
             pltpu.VMEM((2, rows * 8, 128), F32),
             pltpu.VMEM((every, w_g.shape[2]), BF16),
-            pltpu.VMEM((every, 32), F32),
-            dma((7,)),
+            pltpu.VMEM((every, w_g.shape[2]), BF16),
+            pltpu.VMEM((8, every, 128), F32),
+            pltpu.VMEM((rows, 128), F32),
+            pltpu.VMEM((4, 2, 16, 128), F32),
+            dma((28,)),
             dma((2, 2)),
             dma,
+            dma((3,)),
+            dma((3,)),
             dma((3, chunks)),
             dma((3, chunks)),
             dma((3, chunks)),
@@ -353,7 +459,7 @@
             dma((chunks,)),
         ],
         compiler_params=pltpu.CompilerParams(collective_id=0, has_side_effects=True, vmem_limit_bytes=67043328),
-    )(hidden, k_rows, v_rows, w_q, w_k, w_v, w_o, w_g, w_u, w_d, cos, sin, time_mask, multi_hot, *gains, router)
+    )(hidden, k_rows, v_rows, w_q, w_k, w_v, w_o, w_g, w_u, w_d, rotation, positions, ids, *gains, router)
 
 
 def solution(mesh):
@@ -371,20 +477,14 @@
         micro, tokens, width = hidden_in.shape
         rows = MICRO_PER_CHUNK * tokens
         chunks = micro // MICRO_PER_CHUNK
-        pos = seq_pos.reshape(micro * tokens, 1)
-        lanes = jnp.arange(128)
         half = 32
-        inv_freq = THETA ** (-jnp.arange(half, dtype=F32) / half)
-        angles = pos.astype(F32) * jnp.tile(inv_freq, 4)[None, :]
-        cos = jnp.cos(angles)
-        sin = jnp.where(lanes % 64 < 32, -1.0, 1.0) * jnp.sin(angles)
-        time_mask = (lanes[None, :] // 8 < pos).astype(F32)
-        ids = lax.all_gather(expert_ids[0], "ep", axis=0)
-        ids = ids.reshape(4, chunks, rows, 8).transpose(1, 0, 2, 3).reshape(chunks * 4 * rows, 8)
-        multi_hot = jnp.sum((ids[:, :, None] == jnp.arange(32)[None, None, :]).astype(F32), axis=1)
-        gains = (attn_gain.astype(F32), mlp_gain.astype(F32), final_gain.astype(F32).reshape(1, width))
+        inv_freq = (THETA ** (-np.arange(half) / half)).astype(np.float32)
+        angles = (np.arange(1, 17, dtype=np.float32)[:, None] * np.tile(inv_freq, 4)[None, :]).astype(np.float32)
+        sign = np.where(np.arange(128) % 64 < 32, -1.0, 1.0)
+        rotation = jnp.asarray(np.stack([np.cos(angles), sign * np.sin(angles)]).astype(np.float32))
+        gains = (attn_gain, mlp_gain, final_gain)
         weights = (w_query[0], w_key[0], w_value[0], w_out[0], w_gate[0], w_up[0], w_down[0])
-        out, k_new, v_new = run_stack((chunks, rows, stages), hidden_in.reshape(chunks, rows, width), k_cache.reshape(-1, 64), v_cache.reshape(-1, 64), weights, cos, sin, time_mask, multi_hot, gains, w_router[0].T)
+        out, k_new, v_new = place(run_stack((chunks, rows, stages), hidden_in.reshape(chunks, rows, width), k_cache.reshape(-1, 64), v_cache.reshape(-1, 64), weights, rotation, seq_pos.T, expert_ids[0].transpose(1, 2, 0), gains, w_router[0].T))
         new_shape = k_cache.shape[:3] + k_cache.shape[4:]
         return out.reshape(hidden_in.shape), k_new.reshape(new_shape), v_new.reshape(new_shape)
 

time: 268 us -> 221 us (0.82)
  Pallas kernels: 245 us -> 220 us
  local copies, waits for them, and re-layouts: 8.96 us -> 0 us
  blocking collectives: 7.27 us -> 0 us
  other arithmetic: 6.3 us -> 0 us
    pallas_call x1, Pallas kernels: 245 us -> 217 us  [run_stack(): pl.pallas_call(functools.partial(stack_kernel, cfg), out_shape=(jax.Shape...]
    all_gather x1 -> x0, blocking collectives: 7.27 us -> none  [device_fn(): ids = lax.all_gather(expert_ids[0], 'ep', axis=0)]
    unnamed x4 -> x0, local copies, waits for them, and re-layouts: 7.03 us -> none
    convert_element_type x4 -> x0, other arithmetic: 3.35 us -> none  [the longest x1 1.28 us: device_fn(): mlp_gain.astype(F32)]
    pallas_call x0 -> x1, Pallas kernels: none -> 3.03 us  [place(): pl.pallas_call(place_kernel, out_shape=tuple((jax.ShapeDtypeStruct(arr.sh...]
where the time goes in v2:
time: 221 us; the launch traced here: 220 us
  Pallas kernels  220 us (100%)
    pallas_call x1, Pallas kernels, run_stack(): pl.pallas_call(functools.partial(stack_kernel, cfg), out_shape=(jax.Shape...  217 us

profile of v2, /device:TPU:0, one launch (start us, length us, event | category | flops | bytes accessed | tf_op | source)
XLA Modules:
  0.0 220.4 jit_solution(7418494727945011935)
XLA Ops:
  0.6 216.7 %shard_map.184 = (bf16[12,32,1024]{2,1,0:T(8,128)(2,1)}, bf16[3072,64]{1,0:T(8,128)(2,1)}, bf16[3072,64]{1,0:T(8,128)(2,1)}) custom-call(bf16[12,32,1024]{2,1,0:T(8,128)(2,1)} %bitcast.29, bf16[49152,64]{1,0:T(8,128)(2,1)} %bitcast.20, bf16[49152,64]{1,0:T(8,128)(2,1)} %bitcast.21, bf16[1024,1024]{1,0:T(8,128)(2,1)} %bitcast.25, bf16[1024,512]{1,0:T(8,128)(2,1)} %bitcast.27, ...), custom_call_target="tpu_custom_call" | custom-call | tf_op jit(solution)/shard_map/pallas_call | solution.py:415
  217.4 3.0 %shard_map.185 = (bf16[12,32,1024]{2,1,0:T(8,128)(2,1)}, bf16[3072,64]{1,0:T(8,128)(2,1)}, bf16[3072,64]{1,0:T(8,128)(2,1)}) custom-call(bf16[12,32,1024]{2,1,0:T(8,128)(2,1)} %get-tuple-element.9.a_ref, bf16[3072,64]{1,0:T(8,128)(2,1)} %get-tuple-element.10.b_ref, bf16[3072,64]{1,0:T(8,128)(2,1)} %get-tuple-element.11.c_ref), custom_call_target="tpu_custom_call" | custom-call | tf_op jit(solution)/shard_map/pallas_call | solution.py:397

commit v3 on v2

--- a/solution.py
+++ b/solution.py
@@ -11,7 +11,6 @@
 THETA = 1000000.0
 EPS = 1e-05
 MICRO_PER_CHUNK = 2
-UNROLL = 4
 MESH = pl.DeviceIdType.MESH
 F32 = jnp.float32
 BF16 = jnp.bfloat16
@@ -47,6 +46,19 @@
     def block(dev):
         return pl.ds(pl.multiple_of(dev * rows, rows), rows)
 
+    def guard(steady, pred):
+        return (lambda fn: fn()) if steady else pl.when(pred)
+
+    def repeat(steady, first, count):
+        def run(fn):
+            if not steady:
+                pl.loop(first, first + count)(fn)
+            else:
+                for step in range(first, first + count):
+                    fn(step)
+
+        return run
+
     attn_w = [pltpu.make_async_copy(src, dst, w_sem.at[i]) for i, (src, dst) in enumerate(((wq_hbm, wq), (wk_hbm, wk), (wv_hbm, wv), (wo_hbm, wo)))]
     def expert_w(j):
         return [pltpu.make_async_copy(src.at[j], dst.at[j], w_sem.at[4 + which * 8 + j]) for which, (src, dst) in enumerate(((wg_hbm, wg), (wu_hbm, wu), (wd_hbm, wd)))]
@@ -117,25 +129,26 @@
         turned = jnp.where(first_part, pltpu.roll(vals, 96, 1), pltpu.roll(vals, 32, 1))
         return rounded(vals * cos + turned * sin)
 
-    def project(c):
+    def project(c, steady):
 
         @pl.when(stage > 0)
         def _():
             pp_copy(c).wait_recv()
 
-        @pl.when((stage == 0) & (c == 0))
-        def _():
-            hid_copy.wait()
-
-        @pl.when(c == 0)
-        def _():
-            for copy in attn_w:
-                copy.wait()
-
-            @pl.loop(0, 8)
-            def _(j):
-                for copy in expert_w(j):
-                    copy.start()
+        if not steady:
+            @pl.when((stage == 0) & (c == 0))
+            def _():
+                hid_copy.wait()
+
+            @pl.when(c == 0)
+            def _():
+                for copy in attn_w:
+                    copy.wait()
+
+                @pl.loop(0, 8)
+                def _(j):
+                    for copy in expert_w(j):
+                        copy.start()
 
         @pl.when(c + 1 < chunks)
         def _():
@@ -178,19 +191,19 @@
         ko_ref[new_span, :] = kn[0, :, :64].astype(BF16)
         vo_ref[new_span, :] = kn[1, :, :64].astype(BF16)
 
-    def attend(c):
+    def attend(c, steady):
         slot = lax.rem(c, 2)
         for copy in kv_copies(c):
             copy.wait()
 
-        @pl.loop(0, rows // 8, unroll=UNROLL)
+        @repeat(steady, 0, rows // 8)
         def _(g):
-            heads = pl.ds(pl.multiple_of(g * 128, 128), 128)
+            heads = pl.ds(g * 128 if steady else pl.multiple_of(g * 128, 128), 128)
             q_f32 = q2[heads, :64]
             q_bf = q_f32.astype(BF16)
             scores = []
             for b in range(8):
-                keys = kbuf[slot, pl.ds(pl.multiple_of((g * 8 + b) * 128, 128), 128), :]
+                keys = kbuf[slot, pl.ds((g * 8 + b) * 128 if steady else pl.multiple_of((g * 8 + b) * 128, 128), 128), :]
                 valid = pos_col[pl.ds(g * 8 + b, 1), :] > slot_of_lane
                 one = dot_t(q_bf[b * 16:(b + 1) * 16], keys) * 0.125
                 scores.append(jnp.where(own_head & valid, one, -jnp.inf))
@@ -204,7 +217,7 @@
             self_w = rounded(self_w / total)
             outs = []
             for b in range(8):
-                vals = vbuf[slot, pl.ds(pl.multiple_of((g * 8 + b) * 128, 128), 128), :]
+                vals = vbuf[slot, pl.ds((g * 8 + b) * 128 if steady else pl.multiple_of((g * 8 + b) * 128, 128), 128), :]
                 outs.append(dot(weight[b * 16:(b + 1) * 16], vals))
             mixed = jnp.concatenate(outs, axis=0) + self_w * v2[heads, :64]
             o2[heads, :64] = mixed
@@ -257,8 +270,8 @@
                 here = slice(f * 256 + v * 128, f * 256 + (v + 1) * 128)
                 part[slot, :, here] += rounded(scale * term[:, v * 128:(v + 1) * 128])
 
-    def expert_pairs(c, first, count):
-        @pl.loop(first, first + count)
+    def expert_pairs(c, first, count, steady):
+        @repeat(steady, first, count)
         def _(t):
             gate_up(c, 2 * t + 1, act_odd)
             down(c, 2 * t, act_even)
@@ -297,37 +310,36 @@
             for target in range(last):
                 bc_copy(c, target).start()
 
-    @pl.loop(0, chunks + 2)
-    def _(i):
-        @pl.when(i < chunks)
-        def _():
-            project(i)
-
-        @pl.when(i >= 2)
+    def trip(i, steady):
+        has_moe = (i >= 1) & (i <= chunks)
+
+        @guard(steady, i < chunks)
+        def _():
+            project(i, steady)
+
+        @guard(steady, i >= 2)
         def _():
             chip_sum(i - 2)
 
-        has_moe = (i >= 1) & (i <= chunks)
-
-        @pl.when(has_moe)
+        @guard(steady, has_moe)
         def _():
             ag_copy(1, i - 1).wait_recv()
             ag_copy(2, i - 1).start()
 
-        @pl.when(i < chunks)
-        def _():
-            attend(i)
-
-        @pl.when(has_moe)
+        @guard(steady, i < chunks)
+        def _():
+            attend(i, steady)
+
+        @guard(steady, has_moe)
         def _():
             c = i - 1
-
-            @pl.when(c == 0)
-            def _():
-                for which in range(3):
-                    bit_copy(which).wait_recv()
-
-            @pl.when(c >= 2)
+            if not steady:
+                @pl.when(c == 0)
+                def _():
+                    for which in range(3):
+                        bit_copy(which).wait_recv()
+
+            @guard(steady, c >= 2)
             def _():
                 for which in range(3):
                     rs_copy(which, c - 2).wait_send()
@@ -337,32 +349,45 @@
             ag_copy(2, c).wait_recv()
             gates(c)
 
-            @pl.when(c == 0)
-            def _():
-                loading_experts(c)
-
-            @pl.when(c > 0)
+            if not steady:
+                @pl.when(c == 0)
+                def _():
+                    loading_experts(c)
+
+            @guard(steady, c > 0)
             def _():
                 gate_up(c, 0, act_even)
-                expert_pairs(c, 0, 2)
-
-        @pl.when(i >= 2)
+                expert_pairs(c, 0, 2, steady)
+
+        @guard(steady, i >= 2)
         def _():
             finish(i - 2)
 
-        @pl.when(has_moe)
+        @guard(steady, has_moe)
         def _():
             c = i - 1
 
-            @pl.when(c > 0)
+            @guard(steady, c > 0)
             def _():
-                expert_pairs(c, 2, 1)
+                expert_pairs(c, 2, 1, steady)
                 gate_up(c, 7, act_odd)
                 down(c, 6, act_even)
                 down(c, 7, act_odd)
 
             rs_copy(1, c).start()
             rs_copy(0, c).start()
+
+    @pl.loop(0, chunks + 2)
+    def _(i):
+        settled = (i >= 3) & (i < chunks)
+
+        @pl.when(settled)
+        def _():
+            trip(i, True)
+
+        @pl.when(jnp.logical_not(settled))
+        def _():
+            trip(i, False)
 
     for which in range(3):
         bit_copy(which).wait_send()

time: 221 us -> 220 us (level)
  no operation moved by 1% of the time
where the time goes in v3:
time: 220 us; the launch traced here: 219 us
  Pallas kernels  219 us (100%)
    pallas_call x1, Pallas kernels, run_stack(): pl.pallas_call(functools.partial(stack_kernel, cfg), out_shape=(jax.Shape...  216 us

profile of v3, /device:TPU:0, one launch (start us, length us, event | category | flops | bytes accessed | tf_op | source)
XLA Modules:
  0.0 219.3 jit_solution(7554177927598016328)
XLA Ops:
  0.6 215.6 %shard_map.184 = (bf16[12,32,1024]{2,1,0:T(8,128)(2,1)}, bf16[3072,64]{1,0:T(8,128)(2,1)}, bf16[3072,64]{1,0:T(8,128)(2,1)}) custom-call(bf16[12,32,1024]{2,1,0:T(8,128)(2,1)} %bitcast.29, bf16[49152,64]{1,0:T(8,128)(2,1)} %bitcast.20, bf16[49152,64]{1,0:T(8,128)(2,1)} %bitcast.21, bf16[1024,1024]{1,0:T(8,128)(2,1)} %bitcast.25, bf16[1024,512]{1,0:T(8,128)(2,1)} %bitcast.27, ...), custom_call_target="tpu_custom_call" | custom-call | tf_op jit(solution)/shard_map/pallas_call | solution.py:440
  216.3 3.0 %shard_map.185 = (bf16[12,32,1024]{2,1,0:T(8,128)(2,1)}, bf16[3072,64]{1,0:T(8,128)(2,1)}, bf16[3072,64]{1,0:T(8,128)(2,1)}) custom-call(bf16[12,32,1024]{2,1,0:T(8,128)(2,1)} %get-tuple-element.9.a_ref, bf16[3072,64]{1,0:T(8,128)(2,1)} %get-tuple-element.10.b_ref, bf16[3072,64]{1,0:T(8,128)(2,1)} %get-tuple-element.11.c_ref), custom_call_target="tpu_custom_call" | custom-call | tf_op jit(solution)/shard_map/pallas_call | solution.py:422
